TPU v7x, 32 devices: a whole 2x2x4 slice. The times are simulated.
32 devices in a mesh: groups: 2 (over x), patch: 16 (over z, y, core).
Axes of the slice: x: 2, y: 2, z: 4, core: 2. Of those that a mesh axis runs over, the one named last changes fastest.
Arguments:
- tokens: bfloat16 [16384, 1152], P(('groups', 'patch')), parts along dimension 0, may hold values from -6 to 6
- stale_kv: bfloat16 [16384, 1152], P(('groups', 'patch')), parts along dimension 0, may hold values from -40 to 40, as said below
- mod_table: float32 [6, 1152], replicated, may hold values from -2 to 3
- mod_mix: float32 [6, 1152], replicated, may hold values from -3 to 3
- timestep: int32 [2], P('groups'), parts along dimension 0, may hold values from 0 to 999
- frame_order: int32 [8], P('groups'), parts along dimension 0, may hold values from 0 to 3, each once
- spatial_qkv: bfloat16 [3, 1152, 576], replicated, may hold values from -0.1875 to 0.1875
- spatial_out: bfloat16 [576, 1152], replicated, may hold values from -0.25 to 0.25
- temporal_qkv: bfloat16 [3, 1152, 576], replicated, may hold values from -0.1875 to 0.1875
- temporal_out: bfloat16 [576, 1152], replicated, may hold values from -0.25 to 0.25
Outputs:
- block_out: float32 [16384, 1152], P(('groups', 'patch')), parts along dimension 0
There are 2 independent parts, one for each index of `groups`. A program takes and returns all parts, laid end to end along the dimension named above; an argument that names none is the same for every part. Nothing has to cross between parts.
Inputs may be any that keep to these rules, and one draw needn't show every extreme that they name: `frame_order`: a permutation of the 4 time positions. `stale_kv`: previous step's keys and values.
All inputs are finite; a program needn't handle non-finite values.
Results may differ from a plain program's by a relative error of at most 0.013.
The roundings to bfloat16 on the way count: a program that leaves them out, or rounds other values in their place, can miss the bound.
Values may be sent and summed in bfloat16 or wider, within the bound.
A program may use at most 128 MiB of HBM per device.

v0:
```python
import functools
import math

import jax
import jax.numpy as jnp
from jax import lax
from jax.experimental import pallas as pl
from jax.experimental.pallas import tpu as pltpu
from jax.sharding import PartitionSpec as P

HEADS = 16
LANES = 128

epsilon = 1e-06


def normalize(activations):
    row_mean = jnp.mean(activations, axis=-1, keepdims=True)
    centered = activations - row_mean
    variance = jnp.mean(centered * centered, axis=-1, keepdims=True)
    return centered * lax.rsqrt(variance + epsilon)


def sinusoid(position, feature_width):
    half_width = feature_width // 2
    frequencies = jnp.exp(
        -math.log(10000.0) * jnp.arange(half_width, dtype=jnp.float32) / half_width
    )
    angles = jnp.asarray(position).astype(jnp.float32)[..., None] * frequencies
    return jnp.concatenate([jnp.sin(angles), jnp.cos(angles)], axis=-1)


def up_to_lanes(count):
    return -(-count // LANES) * LANES


def window(first, count):
    start, stop = first // LANES * LANES, up_to_lanes(first + count)
    lane = lax.broadcasted_iota(jnp.int32, (1, stop - start), 1) + start
    return start, stop, (lane >= first) & (lane < first + count)


def head_scores(q_rows, kv_refs, head, head_dim):
    start, stop, own = window(head * head_dim, head_dim)
    q_head = jnp.where(own, q_rows[:, start:stop], jnp.zeros((), q_rows.dtype))
    return [
        lax.dot_general(
            q_head, kv[:, start:stop], (((1,), (1,)), ((), ())), preferred_element_type=jnp.float32
        )
        for kv in kv_refs
    ]


def row_max(scores):
    top = scores[0]
    for more in scores[1:]:
        top = jnp.maximum(top, more)
    return jnp.max(top, axis=-1, keepdims=True)


def weigh(scores, top, kv_refs, head, head_dim, width_win):
    factor = head_dim**-0.5 * math.log2(math.e)
    exps = [jnp.exp2((part - top) * factor) for part in scores]
    total = exps[0]
    for more in exps[1:]:
        total = total + more
    total = jnp.sum(total, axis=-1, keepdims=True)
    start, stop, own = window(width_win + head * head_dim, head_dim)
    mixed = None
    for part, kv in zip(exps, kv_refs):
        term = jnp.dot(
            part.astype(jnp.bfloat16), kv[:, start:stop], preferred_element_type=jnp.float32
        )
        mixed = term if mixed is None else mixed + term
    return total, jnp.where(own, mixed, 0.0), start, stop


def near_rows(head_dim, width_win, q_rows, kv_refs, acc, top_ref, sum_ref, at, count):
    base = width_win // LANES * LANES
    heads = width_win // head_dim
    here = pl.ds(at, count)
    acc[here] = jnp.zeros((count,) + acc.shape[1:], acc.dtype)
    scores = head_scores(q_rows, kv_refs, 0, head_dim)
    for head in range(heads):
        later = head_scores(q_rows, kv_refs, head + 1, head_dim) if head + 1 < heads else None
        top = row_max(scores)
        total, mixed, start, stop = weigh(scores, top, kv_refs, head, head_dim, width_win)
        acc[here, :, start - base : stop - base] += mixed.reshape(count, -1, stop - start)
        top_ref[here, :, head : head + 1] = top.reshape(count, -1, 1)
        sum_ref[here, :, head : head + 1] = total.reshape(count, -1, 1)
        scores = later


def far_message(head_dim, width_win, q_rows, kv_refs):
    base = width_win // LANES * LANES
    heads = width_win // head_dim
    tiles = [None] * ((2 * width_win - base) // LANES)
    lane = lax.broadcasted_iota(jnp.int32, (1, LANES), 1)
    stats = jnp.zeros((q_rows.shape[0], LANES), jnp.float32)
    scores = head_scores(q_rows, kv_refs, 0, head_dim)
    for head in range(heads):
        later = head_scores(q_rows, kv_refs, head + 1, head_dim) if head + 1 < heads else None
        top = row_max(scores)
        total, mixed, start, stop = weigh(scores, top, kv_refs, head, head_dim, width_win)
        own = lane % heads == head
        stats = jnp.where(own & (lane < 3 * heads), top, stats)
        stats = jnp.where(own & (lane >= 3 * heads) & (lane < 6 * heads), total, stats)
        for tile in range((stop - start) // LANES):
            at = (start - base) // LANES + tile
            piece = mixed[:, tile * LANES : (tile + 1) * LANES]
            tiles[at] = piece if tiles[at] is None else tiles[at] + piece
        scores = later
    high = stats.astype(jnp.bfloat16).astype(jnp.float32)
    middle = (stats - high).astype(jnp.bfloat16).astype(jnp.float32)
    low = stats - high - middle
    part = lane // heads % 3
    split = jnp.where(part == 0, high, jnp.where(part == 1, middle, low))
    tiles[0] = jnp.where(lane < 6 * heads, split, tiles[0])
    return jnp.concatenate(tiles, axis=1).astype(jnp.bfloat16)


def join(head_dim, width_win, message, acc, top, total):
    base = width_win // LANES * LANES
    heads = width_win // head_dim
    factor = head_dim**-0.5 * math.log2(math.e)
    source = lax.broadcasted_iota(jnp.int32, (LANES, LANES), 0)
    target = lax.broadcasted_iota(jnp.int32, (LANES, LANES), 1)
    wanted = jnp.where(source < 3 * heads, source % heads, heads + source % heads)
    picks = ((source < 6 * heads) & (target == wanted)).astype(jnp.bfloat16)
    stats = jnp.dot(message[:, :LANES], picks, preferred_element_type=jnp.float32)
    tiles = [None] * ((2 * width_win - base) // LANES)
    for head in range(heads):
        near_top, far_top = top[:, head : head + 1], stats[:, head : head + 1]
        best = jnp.maximum(near_top, far_top)
        near_part = jnp.exp2((near_top - best) * factor)
        far_part = jnp.exp2((far_top - best) * factor)
        far_sum = stats[:, heads + head : heads + head + 1]
        inverse = 1.0 / (total[:, head : head + 1] * near_part + far_sum * far_part)
        start, stop, own = window(width_win + head * head_dim, head_dim)
        here = slice(start - base, stop - base)
        near_share = acc[:, here] * jnp.where(own, near_part * inverse, 0.0)
        far_share = message[:, here].astype(jnp.float32) * jnp.where(own, far_part * inverse, 0.0)
        share = near_share + far_share
        for tile in range((stop - start) // LANES):
            at = (start - base) // LANES + tile
            piece = share[:, tile * LANES : (tile + 1) * LANES]
            tiles[at] = piece if tiles[at] is None else tiles[at] + piece
    return jnp.concatenate(tiles, axis=1).astype(jnp.bfloat16)


def spatial_finish(mixed, tokens, out_weight, mod, position):
    projected = jnp.dot(mixed, out_weight, preferred_element_type=jnp.float32)
    after = tokens.astype(jnp.float32) + mod[2:3] * projected
    temporal_in = normalize(after) * (1.0 + mod[4:5]) + mod[3:4] + position
    return after, temporal_in.astype(jnp.bfloat16)


def times_transposed(rows, weight):
    return lax.dot_general(
        rows, weight, (((1,), (1,)), ((), ())), preferred_element_type=jnp.float32
    )


def temporal_rows(head_dim, rows, weight, frames):
    width_win = weight.shape[0] // 3
    count = rows.shape[0]
    pixels = count // frames
    q, k, v = (
        times_transposed(rows, weight[part * width_win : (part + 1) * width_win]).astype(jnp.bfloat16)
        for part in range(3)
    )
    feature = lax.broadcasted_iota(jnp.int32, (width_win, LANES), 0)
    head = lax.broadcasted_iota(jnp.int32, (width_win, LANES), 1)
    gather = ((feature >= head * head_dim) & (feature < (head + 1) * head_dim)).astype(jnp.bfloat16)
    feature = lax.broadcasted_iota(jnp.int32, (LANES, width_win), 1)
    head = lax.broadcasted_iota(jnp.int32, (LANES, width_win), 0)
    spread = ((feature >= head * head_dim) & (feature < (head + 1) * head_dim)).astype(jnp.bfloat16)
    k_wide, v_wide = k.astype(jnp.float32), v.astype(jnp.float32)
    outs = []
    for frame in range(frames):
        q_frame = q[frame * pixels : (frame + 1) * pixels].astype(jnp.float32)
        products = jnp.concatenate(
            [q_frame * k_wide[g * pixels : (g + 1) * pixels] for g in range(frames)], axis=0
        )
        high = products.astype(jnp.bfloat16)
        low = (products - high.astype(jnp.float32)).astype(jnp.bfloat16)
        scores = jnp.dot(high, gather, preferred_element_type=jnp.float32) + jnp.dot(
            low, gather, preferred_element_type=jnp.float32
        )
        scores = [scores[g * pixels : (g + 1) * pixels] * head_dim**-0.5 for g in range(frames)]
        top = functools.reduce(jnp.maximum, scores)
        exps = [jnp.exp(part - top) for part in scores]
        inverse = 1.0 / functools.reduce(jnp.add, exps)
        weights = jnp.concatenate([part * inverse for part in exps], axis=0).astype(jnp.bfloat16)
        spread_weights = jnp.dot(weights, spread, preferred_element_type=jnp.float32)
        terms = spread_weights * v_wide
        mixed = functools.reduce(
            jnp.add, [terms[g * pixels : (g + 1) * pixels] for g in range(frames)]
        )
        outs.append(mixed.astype(jnp.bfloat16))
    return outs


def block_kernel(
    head_dim, tokens_hbm, stale_hbm, spatial_w_hbm, spatial_o_hbm, temporal_w_hbm, temporal_o_hbm,
    mod_ref, out_ref, tokens, kv0, kv1, stale, q, q_in, far_out, far_in, spatial_w, spatial_o, temporal_w, temporal_o,
    acc, top, total, leaving, arriving, mixed_out, mixed_in, load_sem, kv_send, kv_recv, far_send, far_recv, in_send,
    in_recv, back_send, back_recv, own_sem,
):
    chunks, frames, pixels, _ = leaving.shape
    rows = frames * pixels
    width_win = temporal_o.shape[0]
    base = width_win // LANES * LANES
    device = lax.axis_index("patch")
    slot, quarter = device // 4, device % 4

    def flip(mask):
        bit = device // mask % 2
        return device + mask - 2 * mask * bit

    def peer(step):
        other = (slot + step) % frames
        return other, other * 4 + quarter

    loads = [
        pltpu.make_async_copy(source, target, load_sem.at[at])
        for at, (source, target) in enumerate(
            [
                (tokens_hbm, tokens),
                (spatial_w_hbm, spatial_w),
                (stale_hbm, stale),
                (spatial_o_hbm, spatial_o.at[width_win - base :]),
                (temporal_w_hbm, temporal_w),
                (temporal_o_hbm, temporal_o),
            ]
        )
    ]
    for load in loads:
        load.start()

    barrier = pltpu.get_barrier_semaphore()
    others = [flip(2), flip(1)] + [peer(step)[1] for step in range(1, frames)]
    for other in others:
        pl.semaphore_signal(
            barrier, inc=1, device_id={"patch": other}, device_id_type=pl.DeviceIdType.MESH
        )
    pl.semaphore_wait(barrier, len(others))

    def remote(source, target, send, recv, other):
        return pltpu.make_async_remote_copy(
            src_ref=source, dst_ref=target, send_sem=send, recv_sem=recv,
            device_id={"patch": other}, device_id_type=pl.DeviceIdType.MESH,
        )

    beside = remote(stale_hbm, kv1, kv_send.at[0], kv_recv.at[0], flip(1))
    beside.start()

    def ask(c):
        return remote(q.at[c], q_in.at[c], far_send.at[0, c], far_recv.at[0, c], flip(2))

    def answer(c):
        return remote(far_out.at[c], far_in.at[c], far_send.at[1, c], far_recv.at[1, c], flip(2))

    spatial_o[: width_win - base] = jnp.zeros((width_win - base, spatial_o.shape[1]), jnp.bfloat16)
    loads[0].wait()
    loads[1].wait()

    def project(c, carry):
        wide = tokens[c].astype(jnp.float32)
        spatial_in = (normalize(wide) * (1.0 + mod_ref[1:2]) + mod_ref[0:1]).astype(jnp.bfloat16)
        here = pl.ds(pl.multiple_of(c * rows, rows), rows)
        fresh_q, fresh_k, fresh_v = (
            times_transposed(spatial_in, spatial_w[part * width_win : (part + 1) * width_win])
            .astype(jnp.bfloat16)
            for part in range(3)
        )
        q[c, :, :width_win] = fresh_q
        q[c, :, width_win:] = jnp.zeros((rows, q.shape[2] - width_win), jnp.bfloat16)
        kv0[here, :width_win] = fresh_k
        kv0[here, width_win:] = fresh_v
        ask(c).start()
        return carry

    lax.fori_loop(0, chunks, project, 0)
    for load in loads[2:]:
        load.wait()
    beside.wait_recv()

    def serve(c):
        ask(c).wait_recv()
        far_out[c] = far_message(head_dim, width_win, q_in[c], (stale, kv1))
        answer(c).start()

    def inward(c, step):
        other, target = peer(step)
        return other, remote(
            leaving.at[c, other], arriving.at[c, slot], in_send.at[c, step], in_recv.at[c, step],
            target,
        )

    def backward(c, step):
        other, target = peer(step)
        return remote(
            mixed_out.at[c, other], mixed_in.at[c, slot], back_send.at[c, step],
            back_recv.at[c, step], target,
        )

    def keep(c):
        return pltpu.make_async_copy(leaving.at[c, slot], arriving.at[c, slot], own_sem.at[0, c])

    def keep_back(c):
        return pltpu.make_async_copy(mixed_out.at[c, slot], mixed_in.at[c, slot], own_sem.at[1, c])

    def own(c):
        near_rows(head_dim, width_win, q[c], (kv0, kv1), acc, top, total, c, 1)
        answer(c).wait_recv()
        mixed = join(head_dim, width_win, far_in[c], acc.at[c], top.at[c], total.at[c])
        after, temporal_in = spatial_finish(
            mixed, tokens[c], spatial_o[...], mod_ref, mod_ref[6:7]
        )
        out_ref[c] = after
        leaving[c] = temporal_in.reshape(frames, pixels, temporal_in.shape[1])
        for step in range(1, frames):
            inward(c, step)[1].start()
        keep(c).start()

    def temporal(c):
        for step in range(1, frames):
            inward(c, step)[1].wait_recv()
        keep(c).wait()
        flat = arriving[c].reshape(rows, arriving.shape[3])
        for frame, mixed in enumerate(temporal_rows(head_dim, flat, temporal_w, frames)):
            mixed_out[c, frame] = mixed
        for step in range(1, frames):
            backward(c, step).start()
        keep_back(c).start()

    def stage(k, carry):
        @pl.when(k < chunks)
        def _():
            serve(k)

        @pl.when((k >= 1) & (k <= chunks))
        def _():
            own(k - 1)

        @pl.when(k >= 2)
        def _():
            temporal(k - 2)

        return carry

    def third(c, carry):
        for step in range(1, frames):
            backward(c, step).wait_recv()
        keep_back(c).wait()
        mixed = mixed_in[c].reshape(rows, width_win)
        projected = jnp.dot(mixed, temporal_o[...], preferred_element_type=jnp.float32)
        out_ref[c] = out_ref[c] + mod_ref[5:6] * projected
        return carry

    lax.fori_loop(0, chunks + 2, stage, 0)
    lax.fori_loop(0, chunks, third, 0)

    def drain(c, carry):
        ask(c).wait_send()
        answer(c).wait_send()
        for step in range(1, frames):
            inward(c, step)[1].wait_send()
            backward(c, step).wait_send()
        return carry

    lax.fori_loop(0, chunks, drain, 0)
    beside.wait_send()


def per_device(
    tokens,
    stale_kv,
    mod_table,
    mod_mix,
    timestep,
    frame_order,
    spatial_qkv,
    spatial_out,
    temporal_qkv,
    temporal_out,
):
    devices = lax.axis_size("patch")
    dev_index = lax.axis_index("patch")
    frames = devices // 4
    frame_slot = dev_index // 4
    row_count, feature_width = tokens.shape
    width_win = spatial_out.shape[0]
    head_dim = feature_width // HEADS
    base = width_win // LANES * LANES
    q_width = up_to_lanes(width_win)
    v_width = 2 * width_win - base

    modulation = mod_table + mod_mix * sinusoid(timestep[0], feature_width)[None, :]
    frame_id = jnp.sum(jnp.where(jnp.arange(frames) == frame_slot, frame_order, 0))
    position = sinusoid(frame_id, feature_width)[None, :]
    mod = jnp.concatenate([modulation, position, jnp.zeros_like(position)], axis=0)
    chunks = max(1, min(4, row_count // (16 * frames)))
    rows = row_count // chunks
    pixels = rows // frames
    transposed = lambda w: jnp.swapaxes(w, 1, 2).reshape(3 * width_win, feature_width)
    flat = (row_count, feature_width)
    chunked = (chunks, rows, feature_width)
    exchanged = (chunks, frames, pixels)
    anywhere = pl.BlockSpec(memory_space=pl.ANY)
    bf16, f32 = jnp.bfloat16, jnp.float32
    out = pl.pallas_call(
        functools.partial(block_kernel, head_dim),
        in_specs=[anywhere] * 6 + [pl.BlockSpec(memory_space=pltpu.VMEM)],
        out_specs=pl.BlockSpec(memory_space=pltpu.VMEM),
        out_shape=jax.ShapeDtypeStruct(chunked, f32),
        scratch_shapes=[
            pltpu.VMEM(chunked, bf16),
            pltpu.VMEM(flat, bf16),
            pltpu.VMEM(flat, bf16),
            pltpu.VMEM(flat, bf16),
            pltpu.VMEM((chunks, rows, q_width), bf16),
            pltpu.VMEM((chunks, rows, q_width), bf16),
            pltpu.VMEM((chunks, rows, v_width), bf16),
            pltpu.VMEM((chunks, rows, v_width), bf16),
            pltpu.VMEM((3 * width_win, feature_width), bf16),
            pltpu.VMEM((v_width, feature_width), bf16),
            pltpu.VMEM((3 * width_win, feature_width), bf16),
            pltpu.VMEM((width_win, feature_width), bf16),
            pltpu.VMEM((chunks, rows, v_width), f32),
            pltpu.VMEM((chunks, rows, LANES), f32),
            pltpu.VMEM((chunks, rows, LANES), f32),
            pltpu.VMEM(exchanged + (feature_width,), bf16),
            pltpu.VMEM(exchanged + (feature_width,), bf16),
            pltpu.VMEM(exchanged + (width_win,), bf16),
            pltpu.VMEM(exchanged + (width_win,), bf16),
            pltpu.SemaphoreType.DMA((6,)),
            pltpu.SemaphoreType.DMA((1,)),
            pltpu.SemaphoreType.DMA((1,)),
            pltpu.SemaphoreType.DMA((2, chunks)),
            pltpu.SemaphoreType.DMA((2, chunks)),
            pltpu.SemaphoreType.DMA((chunks, frames)),
            pltpu.SemaphoreType.DMA((chunks, frames)),
            pltpu.SemaphoreType.DMA((chunks, frames)),
            pltpu.SemaphoreType.DMA((chunks, frames)),
            pltpu.SemaphoreType.DMA((2, chunks)),
        ],
        compiler_params=pltpu.CompilerParams(
            collective_id=0, has_side_effects=True, vmem_limit_bytes=60 * 1024 * 1024
        ),
        name="denoising_block",
    )(
        tokens.reshape(chunked), stale_kv, transposed(spatial_qkv), spatial_out,
        transposed(temporal_qkv), temporal_out, mod,
    )
    return out.reshape(flat)


def solution(mesh):
    return jax.shard_map(
        per_device,
        mesh=mesh,
        in_specs=(
            P(("groups", "patch"), None),
            P(("groups", "patch"), None),
            P(),
            P(),
            P("groups"),
            P("groups"),
            P(),
            P(),
            P(),
            P(),
        ),
        out_specs=P(("groups", "patch"), None),
        check_vma=False,
    )
```

profile of v0, /device:TPU:0, one launch (start us, length us, event | category | flops | bytes accessed | tf_op | source)
XLA Modules:
  0.0 81.4 jit_solution(4406616096205816169)
XLA Ops:
  0.7 1.3 %fusion.6 = s32[]{:T(128)} fusion(s32[4]{0:T(128)} %param.15, s32[]{:T(128)S(6)} %select_n.9), kind=kLoop, calls=%fused_computation.12 | loop fusion | flops 11 | bytes 24 | tf_op jit(solution)/shard_map/reduce_sum | solution.py:401
  2.6 0.1 pad.2.clone
  2.7 0.1 pad_maximum_fusion.1
  2.8 0.1 fusion.2
  2.9 0.1 pad_maximum_fusion
  2.9 0.8 multiply_add_fusion
  3.8 0.7 maximum_maximum_fusion.mod_ref
  4.4 73.7 %denoising_block.1 = f32[4,128,1152]{2,1,0:T(8,128)} custom-call(bf16[4,128,1152]{2,1,0:T(8,128)(2,1)} %bitcast.13, bf16[512,1152]{1,0:T(8,128)(2,1)} %stale_hbm.1, bf16[1728,1152]{1,0:T(8,128)(2,1)} %bitcast.11, bf16[576,1152]{1,0:T(8,128)(2,1)} %spatial_o_hbm.1, bf16[1728,1152]{1,0:T(8,128)(2,1)} %bitcast.12, bf16[576,1152]{1,0:T(8,128)(2,1)} %temporal_o_hbm.1, ...), custom_call_target="tpu_custom_call" | custom-call | tf_op jit(solution)/shard_map/denoising_block/pallas_call | solution.py:413
  78.1 3.2 %copy.13 = f32[512,1152]{1,0:T(8,128)} copy(f32[512,1152]{1,0:T(8,128)} %bitcast.10) | data formatting | bytes 4718592
  (2 shorter events, 0.1 us)
where the time goes:
time: 81.7 us; the launch traced here: 81.4 us
  Pallas kernels  73.7 us (90%)
  local copies, waits for them, and re-layouts  3.3 us (4%)
  other arithmetic  3.04 us (4%)
  between operations  1.33 us (2%)
    pallas_call x1, Pallas kernels, per_device(): pl.pallas_call(functools.partial(block_kernel, head_dim), in_specs=[anywh...  73.7 us
    unnamed x1, local copies, waits for them, and re-layouts  3.22 us

commit v1 on v0

v1 whole, which is shorter than its diff:
```python
import functools
import math

import jax
import jax.numpy as jnp
from jax import lax
from jax.experimental import pallas as pl
from jax.experimental.pallas import tpu as pltpu
from jax.sharding import PartitionSpec as P

HEADS = 16
LANES = 128
PACK = 16

epsilon = 1e-06
bf16, f32 = jnp.bfloat16, jnp.float32


def normalize(activations):
    row_mean = jnp.mean(activations, axis=-1, keepdims=True)
    centered = activations - row_mean
    variance = jnp.mean(centered * centered, axis=-1, keepdims=True)
    return centered * lax.rsqrt(variance + epsilon)


def sinusoid_row(position, width):
    half = width // 2
    lane = lax.broadcasted_iota(jnp.int32, (8, width), 1)
    index = jnp.where(lane < half, lane, lane - half).astype(f32)
    angle = position.astype(f32) * jnp.exp(index * (-math.log(10000.0) / half))
    return jnp.where(lane < half, jnp.sin(angle), jnp.cos(angle))


def up_to(count, unit):
    return -(-count // unit) * unit


def pair_window(pair, head_dim, width):
    first = 2 * head_dim * pair
    return first // LANES * LANES, min(up_to(first + 2 * head_dim, LANES), width)


def outer(a, b):
    return lax.dot_general(a, b, (((1,), (1,)), ((), ())), preferred_element_type=f32)


def pair_scores(queries, keys, pair, head_dim):
    width = queries.shape[0]
    start, stop = pair_window(pair, head_dim, width)
    feature = lax.broadcasted_iota(jnp.int32, (stop - start, LANES), 0) + start
    part = queries[start:stop]
    split = []
    for head in (2 * pair, 2 * pair + 1):
        own = (feature >= head * head_dim) & (feature < (head + 1) * head_dim)
        split.append(part * own.astype(f32).astype(bf16))
    columns = jnp.concatenate(split, axis=1)
    return [jnp.dot(rows[:, start:stop], columns, preferred_element_type=f32) for rows in keys]


def attend(head_dim, queries, keys, values, put):
    width, count = queries.shape
    pairs = width // (2 * head_dim)
    factor = head_dim**-0.5 * math.log2(math.e)
    scores = pair_scores(queries, keys, 0, head_dim)
    for pair in range(pairs):
        later = pair_scores(queries, keys, pair + 1, head_dim) if pair + 1 < pairs else None
        top = functools.reduce(jnp.maximum, [jnp.max(part, axis=0, keepdims=True) for part in scores])
        mixed = None
        for part, value in zip(scores, values):
            weight = jnp.exp2((part - top) * factor).astype(bf16)
            term = jnp.dot(value[pair], weight, preferred_element_type=f32)
            mixed = term if mixed is None else mixed + term
        for side in range(2):
            column = slice(side * count, (side + 1) * count)
            put(
                2 * pair + side,
                mixed[side * head_dim : (side + 1) * head_dim, column],
                top[:, column],
                mixed[2 * head_dim : 2 * head_dim + 1, column],
            )
        scores = later


def block_kernel(
    head_dim, frames, tokens_hbm, stale_hbm, spatial_w_hbm, spatial_o_hbm, temporal_w_hbm, temporal_o_hbm,
    table_ref, mix_ref, timestep_ref, order_ref, out_ref, tokens, spatial_in, k0, kv1, stale, v0, v1, v_stale,
    q, q_in, far_out, far_in, far_stat, stat_in, near, near_stat, spatial_w, spatial_o, temporal_w, temporal_o,
    mod, leaving, arriving, mixed_out, mixed_in, load_sem, kv_send, kv_recv, far_send, far_recv, in_send,
    in_recv, back_send, back_recv,
):
    chunks, _, pixels, _ = leaving.shape
    rows = frames * pixels
    width, feature_width = spatial_o.shape
    heads = width // head_dim
    pairs = heads // 2
    base = width // LANES * LANES
    factor = head_dim**-0.5 * math.log2(math.e)
    device = lax.axis_index("patch")
    slot, quarter = device // 4, device % 4

    def flip(value, mask):
        bit = value // mask % 2
        return value + mask - 2 * mask * bit

    def peer(step):
        other = slot
        mask = 1
        while mask <= step:
            if step & mask:
                other = flip(other, mask)
            mask *= 2
        return other, other * 4 + quarter

    across, beside_me = flip(device, 2), flip(device, 1)

    def load(at, source, target):
        return pltpu.make_async_copy(source, target, load_sem.at[at])

    part_of = lambda ref, part: ref.at[pl.ds(part * width, width)]
    loads = [load(0, tokens_hbm, tokens)]
    loads += [load(1 + part, part_of(spatial_w_hbm, part), part_of(spatial_w, part)) for part in range(3)]
    loads += [
        load(4, stale_hbm, stale),
        load(5, spatial_o_hbm, spatial_o),
        load(6, temporal_w_hbm, temporal_w),
        load(7, temporal_o_hbm, temporal_o),
    ]
    loads[0].start()
    loads[1].start()

    barrier = pltpu.get_barrier_semaphore()
    others = [across, beside_me] + [peer(step)[1] for step in range(1, frames)]
    for other in others:
        pl.semaphore_signal(
            barrier, inc=1, device_id={"patch": other}, device_id_type=pl.DeviceIdType.MESH
        )

    emb = sinusoid_row(timestep_ref[0], feature_width)
    mod[0:6] = table_ref[...] + mix_ref[...] * emb[0:6]
    mod[6:7] = sinusoid_row(order_ref[slot], feature_width)[0:1]
    pl.semaphore_wait(barrier, len(others))

    def remote(source, target, send, recv, other):
        return pltpu.make_async_remote_copy(
            src_ref=source, dst_ref=target, send_sem=send, recv_sem=recv,
            device_id={"patch": other}, device_id_type=pl.DeviceIdType.MESH,
        )

    beside = remote(stale_hbm, kv1, kv_send.at[0], kv_recv.at[0], beside_me)

    def ask(c):
        return remote(q.at[c], q_in.at[c], far_send.at[0, c], far_recv.at[0, c], across)

    def answers(c):
        return (
            remote(far_out.at[c], far_in.at[c], far_send.at[1, c], far_recv.at[1, c], across),
            remote(far_stat.at[c], stat_in.at[c], far_send.at[2, c], far_recv.at[2, c], across),
        )

    loads[0].wait()
    beside.start()
    for one in loads[2:]:
        one.start()
    loads[1].wait()

    group = spatial_in.shape[1]
    per_group = group // rows

    def queries(g, carry):
        wide = tokens[g].astype(f32)
        x = (normalize(wide) * (1.0 + mod[1:2]) + mod[0:1]).astype(bf16)
        spatial_in[g] = x
        fresh = outer(spatial_w[:width], x).astype(bf16)
        for i in range(per_group):
            q[g * per_group + i] = fresh[:, i * rows : (i + 1) * rows]

        @pl.when(g == 0)
        def _():
            for c in range(min(2, chunks)):
                ask(c).start()

        return carry

    ahead = min(2, chunks)
    lax.fori_loop(0, spatial_in.shape[0], queries, 0)
    loads[2].wait()
    loads[3].wait()
    tail = (lax.broadcasted_iota(jnp.int32, (PACK, group), 0) == 0).astype(f32).astype(bf16)

    def keys_values(g, carry):
        x = spatial_in[g]
        here = pl.ds(pl.multiple_of(g * group, group), group)
        k0[here, :] = outer(x, spatial_w[width : 2 * width]).astype(bf16)
        fresh = outer(spatial_w[2 * width :], x).astype(bf16)
        for pair in range(pairs):
            v0[pair, : 2 * head_dim, here] = fresh[2 * head_dim * pair : 2 * head_dim * (pair + 1)]
            for ref in (v0, v1, v_stale):
                ref[pair, 2 * head_dim :, here] = tail
        return carry

    lax.fori_loop(0, spatial_in.shape[0], keys_values, 0)

    def turn(source, target):
        def body(g, carry):
            here = pl.ds(pl.multiple_of(g * group, group), group)
            turned = source[here, base:].T
            for pair in range(pairs):
                at = width - base + 2 * head_dim * pair
                target[pair, : 2 * head_dim, here] = turned[at : at + 2 * head_dim]
            return carry

        lax.fori_loop(0, spatial_in.shape[0], body, 0)

    for one in loads[4:]:
        one.wait()
    turn(stale, v_stale)
    beside.wait_recv()
    turn(kv1, v1)

    def serve(c):
        def put(head, mixed, top, total):
            far_out[c, head * head_dim : (head + 1) * head_dim] = mixed.astype(bf16)
            far_stat[c, head : head + 1] = top
            far_stat[c, heads + head : heads + head + 1] = total

        ask(c).wait_recv()
        attend(head_dim, q_in[c], (stale, kv1), (v_stale, v1), put)
        for one in answers(c):
            one.start()

        @pl.when(c + ahead < chunks)
        def _():
            ask(c + ahead).start()

    def close(c):
        def put(head, mixed, top, total):
            near[c, head * head_dim : (head + 1) * head_dim] = mixed
            near_stat[c, head : head + 1] = top
            near_stat[c, heads + head : heads + head + 1] = total

        attend(head_dim, q[c], (k0, kv1), (v0, v1), put)

    def inward(c, step):
        other, target = peer(step)
        return remote(
            leaving.at[c, other], arriving.at[c, slot], in_send.at[c, step], in_recv.at[c, step], target
        )

    def backward(c, step):
        other, target = peer(step)
        return remote(
            mixed_out.at[c, other], mixed_in.at[c, slot], back_send.at[c, step], back_recv.at[c, step], target
        )

    def join(c):
        for one in answers(c):
            one.wait_recv()
        near_top, near_sum = near_stat[c, :heads], near_stat[c, heads:]
        far_top, far_sum = stat_in[c, :heads], stat_in[c, heads:]
        best = jnp.maximum(near_top, far_top)
        near_part = jnp.exp2((near_top - best) * factor)
        far_part = jnp.exp2((far_top - best) * factor)
        inverse = 1.0 / (near_sum * near_part + far_sum * far_part)
        near_part, far_part = near_part * inverse, far_part * inverse
        shares = []
        for head in range(heads):
            here = slice(head * head_dim, (head + 1) * head_dim)
            shares.append(
                near[c, here] * near_part[head : head + 1]
                + far_in[c, here].astype(f32) * far_part[head : head + 1]
            )
        mixed = jnp.concatenate(shares, axis=0).T.astype(bf16)
        projected = jnp.dot(mixed, spatial_o[...], preferred_element_type=f32)
        after = tokens[c // per_group, pl.ds(pl.multiple_of(c % per_group * rows, rows), rows)].astype(f32)
        after = after + mod[2:3] * projected
        out_ref[c] = after
        temporal_in = normalize(after) * (1.0 + mod[4:5]) + mod[3:4] + mod[6:7]
        leaving[c] = temporal_in.astype(bf16).reshape(frames, pixels, feature_width)
        for step in range(1, frames):
            inward(c, step).start()
        arriving[c, slot] = leaving[c, slot]

    def temporal(c):
        for step in range(1, frames):
            inward(c, step).wait_recv()
        x = arriving[c].reshape(rows, feature_width)
        turned = (heads, head_dim, rows)
        q_all, k_all, v_all = (
            outer(temporal_w[part * width : (part + 1) * width], x).astype(bf16).astype(f32)
            for part in range(3)
        )
        shift = lambda a, step: pltpu.roll(a, (frames - step) * pixels, 1) if step else a
        scores = [
            jnp.sum((q_all * shift(k_all, step)).reshape(turned), axis=1, keepdims=True) * head_dim**-0.5
            for step in range(frames)
        ]
        top = functools.reduce(jnp.maximum, scores)
        exps = [jnp.exp(part - top) for part in scores]
        inverse = 1.0 / functools.reduce(jnp.add, exps)
        mixed = None
        for step, part in enumerate(exps):
            weight = (part * inverse).astype(bf16).astype(f32)
            term = weight * shift(v_all, step).reshape(turned)
            mixed = term if mixed is None else mixed + term
        mixed = mixed.reshape(width, rows).T.astype(bf16)
        mixed_out[c] = mixed.reshape(frames, pixels, width)
        for step in range(1, frames):
            backward(c, step).start()
        mixed_in[c, slot] = mixed_out[c, slot]

    def stage(k, carry):
        @pl.when(k < chunks)
        def _():
            close(k)
            serve(k)

        @pl.when(k >= 3)
        def _():
            temporal(k - 3)

        @pl.when((k >= 1) & (k <= chunks))
        def _():
            join(k - 1)

        return carry

    def third(c, carry):
        for step in range(1, frames):
            backward(c, step).wait_recv()
        mixed = mixed_in[c].reshape(rows, width)
        projected = jnp.dot(mixed, temporal_o[...], preferred_element_type=f32)
        out_ref[c] = out_ref[c] + mod[5:6] * projected
        return carry

    lax.fori_loop(0, chunks + 3, stage, 0)
    lax.fori_loop(0, chunks, third, 0)

    def drain(c, carry):
        ask(c).wait_send()
        for one in answers(c):
            one.wait_send()
        for step in range(1, frames):
            inward(c, step).wait_send()
            backward(c, step).wait_send()
        return carry

    lax.fori_loop(0, chunks, drain, 0)
    beside.wait_send()


def per_device(
    tokens,
    stale_kv,
    mod_table,
    mod_mix,
    timestep,
    frame_order,
    spatial_qkv,
    spatial_out,
    temporal_qkv,
    temporal_out,
):
    frames = lax.axis_size("patch") // 4
    row_count, feature_width = tokens.shape
    width = spatial_out.shape[0]
    head_dim = feature_width // HEADS
    heads = width // head_dim
    pairs = heads // 2
    rows = LANES
    chunks = row_count // rows
    pixels = rows // frames
    group = min(2 * rows, row_count)
    grouped = (row_count // group, group, feature_width)
    turned = lambda w: jnp.swapaxes(w, 1, 2).reshape(3 * width, feature_width)
    flat = (row_count, feature_width)
    chunked = (chunks, rows, feature_width)
    exchanged = (chunks, frames, pixels)
    value_shape = (pairs, 2 * head_dim + PACK, row_count)
    stat_shape = (chunks, 2 * heads, rows)
    anywhere = pl.BlockSpec(memory_space=pl.ANY)
    vmem = pl.BlockSpec(memory_space=pltpu.VMEM)
    smem = pl.BlockSpec(memory_space=pltpu.SMEM)
    out = pl.pallas_call(
        functools.partial(block_kernel, head_dim, frames),
        in_specs=[anywhere] * 6 + [vmem, vmem, smem, smem],
        out_specs=vmem,
        out_shape=jax.ShapeDtypeStruct(chunked, f32),
        scratch_shapes=[
            pltpu.VMEM(grouped, bf16),
            pltpu.VMEM(grouped, bf16),
            pltpu.VMEM((row_count, width), bf16),
            pltpu.VMEM(flat, bf16),
            pltpu.VMEM(flat, bf16),
            pltpu.VMEM(value_shape, bf16),
            pltpu.VMEM(value_shape, bf16),
            pltpu.VMEM(value_shape, bf16),
            pltpu.VMEM((chunks, width, rows), bf16),
            pltpu.VMEM((chunks, width, rows), bf16),
            pltpu.VMEM((chunks, width, rows), bf16),
            pltpu.VMEM((chunks, width, rows), bf16),
            pltpu.VMEM(stat_shape, f32),
            pltpu.VMEM(stat_shape, f32),
            pltpu.VMEM((chunks, width, rows), f32),
            pltpu.VMEM(stat_shape, f32),
            pltpu.VMEM((3 * width, feature_width), bf16),
            pltpu.VMEM((width, feature_width), bf16),
            pltpu.VMEM((3 * width, feature_width), bf16),
            pltpu.VMEM((width, feature_width), bf16),
            pltpu.VMEM((8, feature_width), f32),
            pltpu.VMEM(exchanged + (feature_width,), bf16),
            pltpu.VMEM(exchanged + (feature_width,), bf16),
            pltpu.VMEM(exchanged + (width,), bf16),
            pltpu.VMEM(exchanged + (width,), bf16),
            pltpu.SemaphoreType.DMA((8,)),
            pltpu.SemaphoreType.DMA((1,)),
            pltpu.SemaphoreType.DMA((1,)),
            pltpu.SemaphoreType.DMA((3, chunks)),
            pltpu.SemaphoreType.DMA((3, chunks)),
            pltpu.SemaphoreType.DMA((chunks, frames)),
            pltpu.SemaphoreType.DMA((chunks, frames)),
            pltpu.SemaphoreType.DMA((chunks, frames)),
            pltpu.SemaphoreType.DMA((chunks, frames)),
        ],
        compiler_params=pltpu.CompilerParams(
            collective_id=0, has_side_effects=True, vmem_limit_bytes=60 * 1024 * 1024
        ),
        name="denoising_block",
    )(
        tokens.reshape(grouped), stale_kv, turned(spatial_qkv), spatial_out,
        turned(temporal_qkv), temporal_out, mod_table, mod_mix, timestep, frame_order,
    )
    return out.reshape(flat)


def solution(mesh):
    return jax.shard_map(
        per_device,
        mesh=mesh,
        in_specs=(
            P(("groups", "patch"), None),
            P(("groups", "patch"), None),
            P(),
            P(),
            P("groups"),
            P("groups"),
            P(),
            P(),
            P(),
            P(),
        ),
        out_specs=P(("groups", "patch"), None),
        check_vma=False,
    )
```

time: 81.7 us -> 68.2 us (0.83)
  Pallas kernels: 73.7 us -> 64.1 us
  other arithmetic: 3.04 us -> 0 us
    pallas_call x1, Pallas kernels: 73.7 us -> 64.1 us  [per_device(): pl.pallas_call(functools.partial(block_kernel, head_dim, frames), in_spec...]
    reduce_sum x1 -> x0, other arithmetic: 1.29 us -> none  [per_device(): jnp.sum(jnp.where(jnp.arange(frames) == frame_slot, frame_order, 0))]
    concatenate x3 -> x0, other arithmetic: 0.84 us -> none  [the longest x1 0.69 us: per_device(): jnp.concatenate([modulation, position, jnp.zeros_like(position)], axis=0)]
where the time goes in v1:
time: 68.2 us; the launch traced here: 68 us
  Pallas kernels  64.1 us (94%)
  local copies, waits for them, and re-layouts  3.22 us (5%)
    pallas_call x1, Pallas kernels, per_device(): pl.pallas_call(functools.partial(block_kernel, head_dim, frames), in_spec...  64.1 us
    unnamed x1, local copies, waits for them, and re-layouts  3.22 us

profile of v1, /device:TPU:0, one launch (start us, length us, event | category | flops | bytes accessed | tf_op | source)
XLA Modules:
  0.0 68.0 jit_solution(115500430315771825)
XLA Ops:
  0.7 64.1 %denoising_block.1 = f32[4,128,1152]{2,1,0:T(8,128)} custom-call(bf16[2,256,1152]{2,1,0:T(8,128)(2,1)} %bitcast.11, bf16[512,1152]{1,0:T(8,128)(2,1)} %stale_hbm.1, bf16[1728,1152]{1,0:T(8,128)(2,1)} %bitcast.9, bf16[576,1152]{1,0:T(8,128)(2,1)} %spatial_o_hbm.1, bf16[1728,1152]{1,0:T(8,128)(2,1)} %bitcast.10, bf16[576,1152]{1,0:T(8,128)(2,1)} %temporal_o_hbm.1, ...), custom_call_target="tpu_custom_call" | custom-call | tf_op jit(solution)/shard_map/denoising_block/pallas_call | solution.py:383
  64.8 3.2 %copy.13 = f32[512,1152]{1,0:T(8,128)} copy(f32[512,1152]{1,0:T(8,128)} %bitcast.8) | data formatting | bytes 4718592

commit v2 on v1

--- a/solution.py
+++ b/solution.py
@@ -23,16 +23,21 @@
     return centered * lax.rsqrt(variance + epsilon)
 
 
-def sinusoid_row(position, width):
-    half = width // 2
-    lane = lax.broadcasted_iota(jnp.int32, (8, width), 1)
-    index = jnp.where(lane < half, lane, lane - half).astype(f32)
-    angle = position.astype(f32) * jnp.exp(index * (-math.log(10000.0) / half))
-    return jnp.where(lane < half, jnp.sin(angle), jnp.cos(angle))
-
-
 def up_to(count, unit):
     return -(-count // unit) * unit
+
+
+def sinusoids(positions, width):
+    half = width // 2
+    count = up_to(len(positions), 8)
+    row = lax.broadcasted_iota(jnp.int32, (count, width), 0)
+    lane = lax.broadcasted_iota(jnp.int32, (count, width), 1)
+    where_to = jnp.zeros((count, width), f32)
+    for at, position in enumerate(positions):
+        where_to = jnp.where(row == at, position.astype(f32), where_to)
+    index = jnp.where(lane < half, lane, lane - half).astype(f32)
+    angle = where_to * jnp.exp(index * (-math.log(10000.0) / half))
+    return jnp.where(lane < half, jnp.sin(angle), jnp.cos(angle))
 
 
 def pair_window(pair, head_dim, width):
@@ -83,10 +88,10 @@
 
 def block_kernel(
     head_dim, frames, tokens_hbm, stale_hbm, spatial_w_hbm, spatial_o_hbm, temporal_w_hbm, temporal_o_hbm,
-    table_ref, mix_ref, timestep_ref, order_ref, out_ref, tokens, spatial_in, k0, kv1, stale, v0, v1, v_stale,
+    table_hbm, mix_hbm, order_hbm, timestep, out_ref, table, mix, order, tokens, spatial_in, k0, kv1, stale, v0, v1, v_stale,
     q, q_in, far_out, far_in, far_stat, stat_in, near, near_stat, spatial_w, spatial_o, temporal_w, temporal_o,
-    mod, leaving, arriving, mixed_out, mixed_in, load_sem, kv_send, kv_recv, far_send, far_recv, in_send,
-    in_recv, back_send, back_recv,
+    mod, place, leaving, arriving, ahead_in, part_out, part_in, mixed_out, mixed_in, load_sem, kv_send, kv_recv,
+    far_send, far_recv, ahead_send, ahead_recv, in_send, in_recv, back_send, back_recv,
 ):
     chunks, _, pixels, _ = leaving.shape
     rows = frames * pixels
@@ -125,8 +130,13 @@
         load(6, temporal_w_hbm, temporal_w),
         load(7, temporal_o_hbm, temporal_o),
     ]
-    loads[0].start()
-    loads[1].start()
+    small = [
+        load(8, order_hbm, order),
+        load(9, table_hbm, table),
+        load(10, mix_hbm, mix),
+    ]
+    for one in small + loads[:2]:
+        one.start()
 
     barrier = pltpu.get_barrier_semaphore()
     others = [across, beside_me] + [peer(step)[1] for step in range(1, frames)]
@@ -135,9 +145,11 @@
             barrier, inc=1, device_id={"patch": other}, device_id_type=pl.DeviceIdType.MESH
         )
 
-    emb = sinusoid_row(timestep_ref[0], feature_width)
-    mod[0:6] = table_ref[...] + mix_ref[...] * emb[0:6]
-    mod[6:7] = sinusoid_row(order_ref[slot], feature_width)[0:1]
+    for one in small:
+        one.wait()
+    waves = sinusoids([timestep[0]] + [order[f] for f in range(frames)], feature_width)
+    place[...] = waves
+    mod[0:6] = table[...] + mix[...] * waves[0:1]
     pl.semaphore_wait(barrier, len(others))
 
     def remote(source, target, send, recv, other):
@@ -157,14 +169,28 @@
             remote(far_stat.at[c], stat_in.at[c], far_send.at[2, c], far_recv.at[2, c], across),
         )
 
+    group = spatial_in.shape[1]
+    per_group = group // rows
+    early = ahead_in.shape[0]
+    lead = min(2, chunks)
+    plain = chunks - early
+
+    def send_ahead(c, step):
+        other, target = peer(step)
+        at = pl.multiple_of(c % per_group * rows + other * pixels, pixels)
+        return remote(
+            tokens_hbm.at[c // per_group, pl.ds(at, pixels)], ahead_in.at[c - plain, slot],
+            ahead_send.at[c - plain, step], ahead_recv.at[c - plain, step], target,
+        )
+
+    for c in range(plain, chunks):
+        for step in range(1, frames):
+            send_ahead(c, step).start()
     loads[0].wait()
     beside.start()
     for one in loads[2:]:
         one.start()
     loads[1].wait()
-
-    group = spatial_in.shape[1]
-    per_group = group // rows
 
     def queries(g, carry):
         wide = tokens[g].astype(f32)
@@ -176,12 +202,11 @@
 
         @pl.when(g == 0)
         def _():
-            for c in range(min(2, chunks)):
+            for c in range(lead):
                 ask(c).start()
 
         return carry
 
-    ahead = min(2, chunks)
     lax.fori_loop(0, spatial_in.shape[0], queries, 0)
     loads[2].wait()
     loads[3].wait()
@@ -228,9 +253,9 @@
         for one in answers(c):
             one.start()
 
-        @pl.when(c + ahead < chunks)
-        def _():
-            ask(c + ahead).start()
+        @pl.when(c + lead < chunks)
+        def _():
+            ask(c + lead).start()
 
     def close(c):
         def put(head, mixed, top, total):
@@ -245,6 +270,20 @@
         return remote(
             leaving.at[c, other], arriving.at[c, slot], in_send.at[c, step], in_recv.at[c, step], target
         )
+
+    def inward_part(c, step):
+        other, target = peer(step)
+        return remote(
+            part_out.at[c - plain, other], part_in.at[c - plain, slot], in_send.at[c, step],
+            in_recv.at[c, step], target,
+        )
+
+    def rows_of(c):
+        here = pl.ds(pl.multiple_of(c % per_group * rows, rows), rows)
+        return tokens[c // per_group, here].astype(f32)
+
+    def to_temporal(after, position):
+        return (normalize(after) * (1.0 + mod[4:5]) + mod[3:4] + position).astype(bf16)
 
     def backward(c, step):
         other, target = peer(step)
@@ -270,19 +309,53 @@
                 + far_in[c, here].astype(f32) * far_part[head : head + 1]
             )
         mixed = jnp.concatenate(shares, axis=0).T.astype(bf16)
+
+        @pl.when(c >= plain)
+        def _():
+            part_out[c - plain] = mixed.reshape(frames, pixels, width)
+            for step in range(1, frames):
+                inward_part(c, step).start()
+            part_in[c - plain, slot] = part_out[c - plain, slot]
+
         projected = jnp.dot(mixed, spatial_o[...], preferred_element_type=f32)
-        after = tokens[c // per_group, pl.ds(pl.multiple_of(c % per_group * rows, rows), rows)].astype(f32)
-        after = after + mod[2:3] * projected
+        after = rows_of(c) + mod[2:3] * projected
         out_ref[c] = after
-        temporal_in = normalize(after) * (1.0 + mod[4:5]) + mod[3:4] + mod[6:7]
-        leaving[c] = temporal_in.astype(bf16).reshape(frames, pixels, feature_width)
+
+        @pl.when(c < plain)
+        def _():
+            temporal_in = to_temporal(out_ref[c], place[pl.ds(1 + slot, 1)])
+            leaving[c] = temporal_in.reshape(frames, pixels, feature_width)
+            for step in range(1, frames):
+                inward(c, step).start()
+            arriving[c, slot] = leaving[c, slot]
+
+        @pl.when(c >= plain)
+        def _():
+            here = pl.ds(pl.multiple_of(c % per_group * rows + slot * pixels, pixels), pixels)
+            ahead_in[c - plain, slot] = tokens[c // per_group, here]
+
+    def complete(c):
         for step in range(1, frames):
-            inward(c, step).start()
-        arriving[c, slot] = leaving[c, slot]
+            send_ahead(c, step).wait_recv()
+            inward_part(c, step).wait_recv()
+        part = part_in[c - plain].reshape(rows, width)
+        projected = jnp.dot(part, spatial_o[...], preferred_element_type=f32)
+        after = ahead_in[c - plain].reshape(rows, feature_width).astype(f32) + mod[2:3] * projected
+        position = place[1 : 1 + frames].reshape(frames, 1, feature_width)
+        position = jnp.broadcast_to(position, (frames, pixels, feature_width))
+        filled = to_temporal(after, position.reshape(rows, feature_width))
+        arriving[c] = filled.reshape(frames, pixels, feature_width)
 
     def temporal(c):
-        for step in range(1, frames):
-            inward(c, step).wait_recv()
+        @pl.when(c < plain)
+        def _():
+            for step in range(1, frames):
+                inward(c, step).wait_recv()
+
+        @pl.when(c >= plain)
+        def _():
+            complete(c)
+
         x = arriving[c].reshape(rows, feature_width)
         turned = (heads, head_dim, rows)
         q_all, k_all, v_all = (
@@ -340,8 +413,19 @@
         for one in answers(c):
             one.wait_send()
         for step in range(1, frames):
-            inward(c, step).wait_send()
             backward(c, step).wait_send()
+
+        @pl.when(c < plain)
+        def _():
+            for step in range(1, frames):
+                inward(c, step).wait_send()
+
+        @pl.when(c >= plain)
+        def _():
+            for step in range(1, frames):
+                inward_part(c, step).wait_send()
+                send_ahead(c, step).wait_send()
+
         return carry
 
     lax.fori_loop(0, chunks, drain, 0)
@@ -378,14 +462,16 @@
     value_shape = (pairs, 2 * head_dim + PACK, row_count)
     stat_shape = (chunks, 2 * heads, rows)
     anywhere = pl.BlockSpec(memory_space=pl.ANY)
-    vmem = pl.BlockSpec(memory_space=pltpu.VMEM)
-    smem = pl.BlockSpec(memory_space=pltpu.SMEM)
+    early = min(2, chunks - 1)
     out = pl.pallas_call(
         functools.partial(block_kernel, head_dim, frames),
-        in_specs=[anywhere] * 6 + [vmem, vmem, smem, smem],
-        out_specs=vmem,
+        in_specs=[anywhere] * 9 + [pl.BlockSpec(memory_space=pltpu.SMEM)],
+        out_specs=pl.BlockSpec(memory_space=pltpu.VMEM),
         out_shape=jax.ShapeDtypeStruct(chunked, f32),
         scratch_shapes=[
+            pltpu.VMEM(mod_table.shape, f32),
+            pltpu.VMEM(mod_mix.shape, f32),
+            pltpu.SMEM(frame_order.shape, jnp.int32),
             pltpu.VMEM(grouped, bf16),
             pltpu.VMEM(grouped, bf16),
             pltpu.VMEM((row_count, width), bf16),
@@ -407,27 +493,39 @@
             pltpu.VMEM((3 * width, feature_width), bf16),
             pltpu.VMEM((width, feature_width), bf16),
             pltpu.VMEM((8, feature_width), f32),
+            pltpu.VMEM((up_to(1 + frames, 8), feature_width), f32),
             pltpu.VMEM(exchanged + (feature_width,), bf16),
             pltpu.VMEM(exchanged + (feature_width,), bf16),
+            pltpu.VMEM((early, frames, pixels, feature_width), bf16),
+            pltpu.VMEM((early, frames, pixels, width), bf16),
+            pltpu.VMEM((early, frames, pixels, width), bf16),
             pltpu.VMEM(exchanged + (width,), bf16),
             pltpu.VMEM(exchanged + (width,), bf16),
-            pltpu.SemaphoreType.DMA((8,)),
+            pltpu.SemaphoreType.DMA((11,)),
             pltpu.SemaphoreType.DMA((1,)),
             pltpu.SemaphoreType.DMA((1,)),
             pltpu.SemaphoreType.DMA((3, chunks)),
             pltpu.SemaphoreType.DMA((3, chunks)),
+            pltpu.SemaphoreType.DMA((early, frames)),
+            pltpu.SemaphoreType.DMA((early, frames)),
             pltpu.SemaphoreType.DMA((chunks, frames)),
             pltpu.SemaphoreType.DMA((chunks, frames)),
             pltpu.SemaphoreType.DMA((chunks, frames)),
             pltpu.SemaphoreType.DMA((chunks, frames)),
         ],
         compiler_params=pltpu.CompilerParams(
-            collective_id=0, has_side_effects=True, vmem_limit_bytes=60 * 1024 * 1024
+            collective_id=0, has_side_effects=True, vmem_limit_bytes=44 * 1024 * 1024
         ),
         name="denoising_block",
     )(
-        tokens.reshape(grouped), stale_kv, turned(spatial_qkv), spatial_out,
-        turned(temporal_qkv), temporal_out, mod_table, mod_mix, timestep, frame_order,
+        *(
+            pltpu.with_memory_space_constraint(operand, pltpu.HBM)
+            for operand in (
+                tokens.reshape(grouped), stale_kv, turned(spatial_qkv), spatial_out, turned(temporal_qkv),
+                temporal_out, mod_table, mod_mix, frame_order,
+            )
+        ),
+        timestep,
     )
     return out.reshape(flat)
 

time: 68.2 us -> 58.8 us (0.86)
  Pallas kernels: 64.1 us -> 56.6 us
  local copies, waits for them, and re-layouts: 3.22 us -> 1.41 us
    pallas_call x1, Pallas kernels: 64.1 us -> 56.6 us  [per_device(): pl.pallas_call(functools.partial(block_kernel, head_dim, frames), in_spec...]
    unnamed x1, local copies, waits for them, and re-layouts: 3.22 us -> 1.41 us
where the time goes in v2:
time: 58.8 us; the launch traced here: 58.6 us
  Pallas kernels  56.6 us (96%)
  local copies, waits for them, and re-layouts  1.41 us (2%)
  between operations  0.66 us (1%)
    pallas_call x1, Pallas kernels, per_device(): pl.pallas_call(functools.partial(block_kernel, head_dim, frames), in_spec...  56.6 us
    unnamed x1, local copies, waits for them, and re-layouts  1.41 us

profile of v2, /device:TPU:0, one launch (start us, length us, event | category | flops | bytes accessed | tf_op | source)
XLA Modules:
  0.0 58.6 jit_solution(17499598642801911473)
XLA Ops:
  0.7 56.6 %denoising_block.1 = f32[4,128,1152]{2,1,0:T(8,128)S(1)} custom-call(bf16[2,256,1152]{2,1,0:T(8,128)(2,1)} %bitcast.11, bf16[512,1152]{1,0:T(8,128)(2,1)} %stale_hbm.1, bf16[1728,1152]{1,0:T(8,128)(2,1)} %bitcast.9, bf16[576,1152]{1,0:T(8,128)(2,1)} %spatial_o_hbm.1, bf16[1728,1152]{1,0:T(8,128)(2,1)} %bitcast.10, bf16[576,1152]{1,0:T(8,128)(2,1)} %temporal_o_hbm.1, ...), custom_call_target="tpu_custom_call" | custom-call | tf_op jit(solution)/shard_map/denoising_block/pallas_call | solution.py:466
  57.2 1.4 %copy.13 = f32[512,1152]{1,0:T(8,128)} copy(f32[512,1152]{1,0:T(8,128)S(1)} %bitcast.8) | data formatting | bytes 4718592

commit v3 on v2

--- a/solution.py
+++ b/solution.py
@@ -43,6 +43,22 @@
 def pair_window(pair, head_dim, width):
     first = 2 * head_dim * pair
     return first // LANES * LANES, min(up_to(first + 2 * head_dim, LANES), width)
+
+
+def fold(mixed, frames, parts):
+    rows, width = mixed.shape
+    each = rows // frames // parts
+    split = mixed.reshape(frames, parts, each, width)
+    side = [split[:, part].reshape(frames * each, width) for part in range(parts)]
+    return jnp.concatenate(side, axis=1).reshape(frames, each, parts * width)
+
+
+def unfold(folded, parts):
+    frames, each, wide = folded.shape
+    width = wide // parts
+    flat = folded.reshape(frames * each, wide)
+    side = [flat[:, part * width : (part + 1) * width].reshape(frames, 1, each, width) for part in range(parts)]
+    return jnp.concatenate(side, axis=1).reshape(frames * parts * each, width)
 
 
 def outer(a, b):
@@ -98,6 +114,7 @@
     width, feature_width = spatial_o.shape
     heads = width // head_dim
     pairs = heads // 2
+    parts = mixed_in.shape[3] // width
     base = width // LANES * LANES
     factor = head_dim**-0.5 * math.log2(math.e)
     device = lax.axis_index("patch")
@@ -122,7 +139,7 @@
         return pltpu.make_async_copy(source, target, load_sem.at[at])
 
     part_of = lambda ref, part: ref.at[pl.ds(part * width, width)]
-    loads = [load(0, tokens_hbm, tokens)]
+    loads = [load(0, tokens_hbm.at[0], tokens.at[0])]
     loads += [load(1 + part, part_of(spatial_w_hbm, part), part_of(spatial_w, part)) for part in range(3)]
     loads += [
         load(4, stale_hbm, stale),
@@ -130,12 +147,13 @@
         load(6, temporal_w_hbm, temporal_w),
         load(7, temporal_o_hbm, temporal_o),
     ]
+    rest = [load(11 + g, tokens_hbm.at[g], tokens.at[g]) for g in range(1, tokens.shape[0])]
     small = [
         load(8, order_hbm, order),
         load(9, table_hbm, table),
         load(10, mix_hbm, mix),
     ]
-    for one in small + loads[:2]:
+    for one in small + loads[:2] + rest:
         one.start()
 
     barrier = pltpu.get_barrier_semaphore()
@@ -145,11 +163,6 @@
             barrier, inc=1, device_id={"patch": other}, device_id_type=pl.DeviceIdType.MESH
         )
 
-    for one in small:
-        one.wait()
-    waves = sinusoids([timestep[0]] + [order[f] for f in range(frames)], feature_width)
-    place[...] = waves
-    mod[0:6] = table[...] + mix[...] * waves[0:1]
     pl.semaphore_wait(barrier, len(others))
 
     def remote(source, target, send, recv, other):
@@ -186,28 +199,33 @@
     for c in range(plain, chunks):
         for step in range(1, frames):
             send_ahead(c, step).start()
+    beside.start()
+    for one in small:
+        one.wait()
+    waves = sinusoids([timestep[0]] + [order[f] for f in range(frames)], feature_width)
+    place[...] = waves
+    mod[0:6] = table[...] + mix[...] * waves[0:1]
     loads[0].wait()
-    beside.start()
     for one in loads[2:]:
         one.start()
     loads[1].wait()
 
-    def queries(g, carry):
-        wide = tokens[g].astype(f32)
-        x = (normalize(wide) * (1.0 + mod[1:2]) + mod[0:1]).astype(bf16)
-        spatial_in[g] = x
+    def queries(g, at, count):
+        x = tokens[g, at : at + count].astype(f32)
+        x = (normalize(x) * (1.0 + mod[1:2]) + mod[0:1]).astype(bf16)
+        spatial_in[g, at : at + count] = x
         fresh = outer(spatial_w[:width], x).astype(bf16)
-        for i in range(per_group):
-            q[g * per_group + i] = fresh[:, i * rows : (i + 1) * rows]
-
-        @pl.when(g == 0)
-        def _():
-            for c in range(lead):
+        for i in range(count // rows):
+            c = g * per_group + at // rows + i
+            q[c] = fresh[:, i * rows : (i + 1) * rows]
+            if c < lead:
                 ask(c).start()
 
-        return carry
-
-    lax.fori_loop(0, spatial_in.shape[0], queries, 0)
+    for at in range(0, group, rows):
+        queries(0, at, rows)
+    for g, one in enumerate(rest):
+        one.wait()
+        queries(g + 1, 0, group)
     loads[2].wait()
     loads[3].wait()
     tail = (lax.broadcasted_iota(jnp.int32, (PACK, group), 0) == 0).astype(f32).astype(bf16)
@@ -312,7 +330,7 @@
 
         @pl.when(c >= plain)
         def _():
-            part_out[c - plain] = mixed.reshape(frames, pixels, width)
+            part_out[c - plain] = fold(mixed, frames, parts)
             for step in range(1, frames):
                 inward_part(c, step).start()
             part_in[c - plain, slot] = part_out[c - plain, slot]
@@ -338,7 +356,7 @@
         for step in range(1, frames):
             send_ahead(c, step).wait_recv()
             inward_part(c, step).wait_recv()
-        part = part_in[c - plain].reshape(rows, width)
+        part = unfold(part_in[c - plain], parts)
         projected = jnp.dot(part, spatial_o[...], preferred_element_type=f32)
         after = ahead_in[c - plain].reshape(rows, feature_width).astype(f32) + mod[2:3] * projected
         position = place[1 : 1 + frames].reshape(frames, 1, feature_width)
@@ -376,37 +394,44 @@
             term = weight * shift(v_all, step).reshape(turned)
             mixed = term if mixed is None else mixed + term
         mixed = mixed.reshape(width, rows).T.astype(bf16)
-        mixed_out[c] = mixed.reshape(frames, pixels, width)
+        mixed_out[c] = fold(mixed, frames, parts)
         for step in range(1, frames):
             backward(c, step).start()
         mixed_in[c, slot] = mixed_out[c, slot]
 
-    def stage(k, carry):
-        @pl.when(k < chunks)
-        def _():
-            close(k)
-            serve(k)
-
-        @pl.when(k >= 3)
-        def _():
-            temporal(k - 3)
-
-        @pl.when((k >= 1) & (k <= chunks))
-        def _():
-            join(k - 1)
-
-        return carry
-
-    def third(c, carry):
+    def third(c):
         for step in range(1, frames):
             backward(c, step).wait_recv()
-        mixed = mixed_in[c].reshape(rows, width)
+        mixed = unfold(mixed_in[c], parts)
         projected = jnp.dot(mixed, temporal_o[...], preferred_element_type=f32)
         out_ref[c] = out_ref[c] + mod[5:6] * projected
+
+    plan = []
+    for k in range(chunks):
+        plan.append((serve, k))
+        if k < chunks - 1:
+            plan.append((close, k))
+        if k >= 3:
+            plan.append((temporal, k - 3))
+        if k >= 1:
+            plan.append((join, k - 1))
+    plan += [(close, chunks - 1), (join, chunks - 1)]
+    plan += [(temporal, c) for c in range(max(0, chunks - 3), chunks)]
+    plan += [(third, c) for c in range(chunks)]
+
+    def turn_of(t, carry):
+        for work in (serve, close, temporal, join, third):
+            turns = [(at, c) for at, (kind, c) in enumerate(plan) if kind is work]
+            due = functools.reduce(jnp.logical_or, [t == at for at, _ in turns])
+            chunk = functools.reduce(lambda other, turn: jnp.where(t == turn[0], turn[1], other), turns, 0)
+
+            @pl.when(due)
+            def _():
+                work(chunk)
+
         return carry
 
-    lax.fori_loop(0, chunks + 3, stage, 0)
-    lax.fori_loop(0, chunks, third, 0)
+    lax.fori_loop(0, len(plan), turn_of, 0)
 
     def drain(c, carry):
         ask(c).wait_send()
@@ -459,10 +484,12 @@
     flat = (row_count, feature_width)
     chunked = (chunks, rows, feature_width)
     exchanged = (chunks, frames, pixels)
+    parts = 2 if width % LANES and pixels % (2 * PACK) == 0 else 1
+    folded = (frames, pixels // parts, parts * width)
     value_shape = (pairs, 2 * head_dim + PACK, row_count)
     stat_shape = (chunks, 2 * heads, rows)
     anywhere = pl.BlockSpec(memory_space=pl.ANY)
-    early = min(2, chunks - 1)
+    early = min(2, max(1, chunks - 1))
     out = pl.pallas_call(
         functools.partial(block_kernel, head_dim, frames),
         in_specs=[anywhere] * 9 + [pl.BlockSpec(memory_space=pltpu.SMEM)],
@@ -497,11 +524,11 @@
             pltpu.VMEM(exchanged + (feature_width,), bf16),
             pltpu.VMEM(exchanged + (feature_width,), bf16),
             pltpu.VMEM((early, frames, pixels, feature_width), bf16),
-            pltpu.VMEM((early, frames, pixels, width), bf16),
-            pltpu.VMEM((early, frames, pixels, width), bf16),
-            pltpu.VMEM(exchanged + (width,), bf16),
-            pltpu.VMEM(exchanged + (width,), bf16),
-            pltpu.SemaphoreType.DMA((11,)),
+            pltpu.VMEM((early,) + folded, bf16),
+            pltpu.VMEM((early,) + folded, bf16),
+            pltpu.VMEM((chunks,) + folded, bf16),
+            pltpu.VMEM((chunks,) + folded, bf16),
+            pltpu.SemaphoreType.DMA((11 + row_count // group,)),
             pltpu.SemaphoreType.DMA((1,)),
             pltpu.SemaphoreType.DMA((1,)),
             pltpu.SemaphoreType.DMA((3, chunks)),

time: 58.8 us -> 55.6 us (0.946)
  Pallas kernels: 56.6 us -> 53.4 us
    pallas_call x1, Pallas kernels: 56.6 us -> 53.4 us  [per_device(): pl.pallas_call(functools.partial(block_kernel, head_dim, frames), in_spec...]
where the time goes in v3:
time: 55.6 us; the launch traced here: 55.5 us
  Pallas kernels  53.4 us (96%)
  local copies, waits for them, and re-layouts  1.41 us (3%)
  between operations  0.66 us (1%)
    pallas_call x1, Pallas kernels, per_device(): pl.pallas_call(functools.partial(block_kernel, head_dim, frames), in_spec...  53.4 us
    unnamed x1, local copies, waits for them, and re-layouts  1.41 us

profile of v3, /device:TPU:0, one launch (start us, length us, event | category | flops | bytes accessed | tf_op | source)
XLA Modules:
  0.0 55.5 jit_solution(9357075845070752202)
XLA Ops:
  0.7 53.4 %denoising_block.1 = f32[4,128,1152]{2,1,0:T(8,128)S(1)} custom-call(bf16[2,256,1152]{2,1,0:T(8,128)(2,1)} %bitcast.11, bf16[512,1152]{1,0:T(8,128)(2,1)} %stale_hbm.1, bf16[1728,1152]{1,0:T(8,128)(2,1)} %bitcast.9, bf16[576,1152]{1,0:T(8,128)(2,1)} %spatial_o_hbm.1, bf16[1728,1152]{1,0:T(8,128)(2,1)} %bitcast.10, bf16[576,1152]{1,0:T(8,128)(2,1)} %temporal_o_hbm.1, ...), custom_call_target="tpu_custom_call" | custom-call | tf_op jit(solution)/shard_map/denoising_block/pallas_call | solution.py:493
  54.1 1.4 %copy.13 = f32[512,1152]{1,0:T(8,128)} copy(f32[512,1152]{1,0:T(8,128)S(1)} %bitcast.8) | data formatting | bytes 4718592

commit v4 on v3

--- a/solution.py
+++ b/solution.py
@@ -163,7 +163,6 @@
             barrier, inc=1, device_id={"patch": other}, device_id_type=pl.DeviceIdType.MESH
         )
 
-    pl.semaphore_wait(barrier, len(others))
 
     def remote(source, target, send, recv, other):
         return pltpu.make_async_remote_copy(
@@ -196,10 +195,13 @@
             ahead_send.at[c - plain, step], ahead_recv.at[c - plain, step], target,
         )
 
-    for c in range(plain, chunks):
-        for step in range(1, frames):
-            send_ahead(c, step).start()
-    beside.start()
+    def meet():
+        pl.semaphore_wait(barrier, len(others))
+        for c in range(plain, chunks):
+            for step in range(1, frames):
+                send_ahead(c, step).start()
+        beside.start()
+
     for one in small:
         one.wait()
     waves = sinusoids([timestep[0]] + [order[f] for f in range(frames)], feature_width)
@@ -218,10 +220,13 @@
         for i in range(count // rows):
             c = g * per_group + at // rows + i
             q[c] = fresh[:, i * rows : (i + 1) * rows]
-            if c < lead:
+            if 0 < c < lead:
                 ask(c).start()
 
-    for at in range(0, group, rows):
+    queries(0, 0, rows)
+    meet()
+    ask(0).start()
+    for at in range(rows, group, rows):
         queries(0, at, rows)
     for g, one in enumerate(rest):
         one.wait()
@@ -406,6 +411,24 @@
         projected = jnp.dot(mixed, temporal_o[...], preferred_element_type=f32)
         out_ref[c] = out_ref[c] + mod[5:6] * projected
 
+    def drain(c):
+        ask(c).wait_send()
+        for one in answers(c):
+            one.wait_send()
+        for step in range(1, frames):
+            backward(c, step).wait_send()
+
+        @pl.when(c < plain)
+        def _():
+            for step in range(1, frames):
+                inward(c, step).wait_send()
+
+        @pl.when(c >= plain)
+        def _():
+            for step in range(1, frames):
+                inward_part(c, step).wait_send()
+                send_ahead(c, step).wait_send()
+
     plan = []
     for k in range(chunks):
         plan.append((serve, k))
@@ -417,10 +440,11 @@
             plan.append((join, k - 1))
     plan += [(close, chunks - 1), (join, chunks - 1)]
     plan += [(temporal, c) for c in range(max(0, chunks - 3), chunks)]
+    plan += [(drain, c) for c in range(chunks)]
     plan += [(third, c) for c in range(chunks)]
 
     def turn_of(t, carry):
-        for work in (serve, close, temporal, join, third):
+        for work in (serve, close, temporal, join, drain, third):
             turns = [(at, c) for at, (kind, c) in enumerate(plan) if kind is work]
             due = functools.reduce(jnp.logical_or, [t == at for at, _ in turns])
             chunk = functools.reduce(lambda other, turn: jnp.where(t == turn[0], turn[1], other), turns, 0)
@@ -432,28 +456,6 @@
         return carry
 
     lax.fori_loop(0, len(plan), turn_of, 0)
-
-    def drain(c, carry):
-        ask(c).wait_send()
-        for one in answers(c):
-            one.wait_send()
-        for step in range(1, frames):
-            backward(c, step).wait_send()
-
-        @pl.when(c < plain)
-        def _():
-            for step in range(1, frames):
-                inward(c, step).wait_send()
-
-        @pl.when(c >= plain)
-        def _():
-            for step in range(1, frames):
-                inward_part(c, step).wait_send()
-                send_ahead(c, step).wait_send()
-
-        return carry
-
-    lax.fori_loop(0, chunks, drain, 0)
     beside.wait_send()
 
 

time: 55.6 us -> 55.3 us (level)
  no operation moved by 1% of the time
where the time goes in v4:
time: 55.3 us; the launch traced here: 55.2 us
  Pallas kernels  53.1 us (96%)
  local copies, waits for them, and re-layouts  1.41 us (3%)
  between operations  0.66 us (1%)
    pallas_call x1, Pallas kernels, per_device(): pl.pallas_call(functools.partial(block_kernel, head_dim, frames), in_spec...  53.1 us
    unnamed x1, local copies, waits for them, and re-layouts  1.41 us

profile of v4, /device:TPU:0, one launch (start us, length us, event | category | flops | bytes accessed | tf_op | source)
XLA Modules:
  0.0 55.2 jit_solution(7668068805711545999)
XLA Ops:
  0.7 53.1 %denoising_block.1 = f32[4,128,1152]{2,1,0:T(8,128)S(1)} custom-call(bf16[2,256,1152]{2,1,0:T(8,128)(2,1)} %bitcast.11, bf16[512,1152]{1,0:T(8,128)(2,1)} %stale_hbm.1, bf16[1728,1152]{1,0:T(8,128)(2,1)} %bitcast.9, bf16[576,1152]{1,0:T(8,128)(2,1)} %spatial_o_hbm.1, bf16[1728,1152]{1,0:T(8,128)(2,1)} %bitcast.10, bf16[576,1152]{1,0:T(8,128)(2,1)} %temporal_o_hbm.1, ...), custom_call_target="tpu_custom_call" | custom-call | tf_op jit(solution)/shard_map/denoising_block/pallas_call | solution.py:495
  53.8 1.4 %copy.13 = f32[512,1152]{1,0:T(8,128)} copy(f32[512,1152]{1,0:T(8,128)S(1)} %bitcast.8) | data formatting | bytes 4718592
